TPU v7x, 32 devices: a whole 2x2x4 slice. The times are simulated.
32 devices in a mesh: groups: 2 (over x), ctx: 16 (over z, y, core).
Axes of the slice: x: 2, y: 2, z: 4, core: 2. Of those that a mesh axis runs over, the one named last changes fastest.
Arguments:
- queries: bfloat16 [256, 2048], P(('groups', 'ctx')), parts along dimension 0, may hold values from -200 to 200
- slab_keys: bfloat16 [256, 2048], P(('groups', 'ctx')), parts along dimension 0, may hold values from -6 to 6
- slab_values: bfloat16 [256, 2048], P(('groups', 'ctx')), parts along dimension 0, may hold values from -6 to 6
- cache_keys: bfloat16 [16384, 2048], P(('groups', 'ctx')), parts along dimension 0, may hold values from -12 to 12
- cache_values: bfloat16 [16384, 2048], P(('groups', 'ctx')), parts along dimension 0, may hold values from -6 to 6
- offset: int32 [2], P('groups'), parts along dimension 0, may hold values from 2048 to 8192
- slab_len: int32 [2], P('groups'), parts along dimension 0, may hold values from 64 to 128
Outputs:
- attended: bfloat16 [256, 2048], P(('groups', 'ctx')), parts along dimension 0
There are 2 independent parts, one for each index of `groups`. A program takes and returns all parts, laid end to end along the dimension named above; each array names one. Nothing has to cross between parts.
All inputs are finite; a program needn't handle non-finite values.
Results may differ from a plain program's by a relative error of at most 0.0081.
Values may be sent and summed in bfloat16 or wider, within the bound.
A program may use at most 128 MiB of HBM per device.

v0:
```python
import jax
import jax.numpy as jnp
from jax import lax
from jax.sharding import PartitionSpec as P

DH = 128
KB = 256
very_low = -1e30


def block_state(query_heads, key_blocks, value_blocks, visible, score_scale):
    scores = (
        jnp.einsum("qhd,gkhd->qghk", query_heads, key_blocks, preferred_element_type=jnp.float32)
        * score_scale
    )
    visible_head = visible[:, :, None, :]
    masked = jnp.where(visible_head, scores, very_low)
    maxima = jnp.max(masked, axis=3)
    weights = jnp.exp(jnp.where(visible_head, scores - maxima[..., None], -jnp.inf))
    totals = jnp.sum(weights, axis=3)
    rounded = weights.astype(jnp.bfloat16)
    products = jnp.einsum(
        "qghk,gkhd->qghd", rounded, value_blocks, preferred_element_type=jnp.float32
    )
    return (maxima, totals, products)


def absorb(running, terms):
    largest, weight_sum, weighted = running
    maxima, totals, products = terms
    new_largest = jnp.maximum(largest, jnp.max(maxima, axis=1))
    old_factor = jnp.exp(largest - new_largest)
    factors = jnp.exp(maxima - new_largest[:, None, :])
    weight_sum = weight_sum * old_factor + jnp.sum(factors * totals, axis=1)
    weighted = weighted * old_factor[..., None] + jnp.sum(factors[..., None] * products, axis=1)
    return (new_largest, weight_sum, weighted)


def body(queries, slab_keys, slab_values, cache_keys, cache_values, offset, slab_len):
    device_rank = lax.axis_index("ctx")
    device_count = lax.axis_size("ctx")
    own_rows = queries.shape[0]
    slab_rows = own_rows * device_count
    cache_rows = cache_keys.shape[0]
    head_count = queries.shape[1] // DH
    score_scale = DH ** (-0.5)
    gathered = lax.all_gather(queries, "ctx", axis=0, tiled=True)
    query_heads = gathered.reshape(slab_rows, head_count, DH)
    running = (
        jnp.full((slab_rows, head_count), very_low, jnp.float32),
        jnp.zeros((slab_rows, head_count), jnp.float32),
        jnp.zeros((slab_rows, head_count, DH), jnp.float32),
    )
    for block_number in range(cache_rows // KB):
        block_start = block_number * KB
        key_blocks = cache_keys[block_start : block_start + KB].reshape(1, KB, head_count, DH)
        value_blocks = cache_values[block_start : block_start + KB].reshape(1, KB, head_count, DH)
        positions = device_rank * cache_rows + block_start + jnp.arange(KB, dtype=jnp.int32)
        visible = jnp.broadcast_to((positions < offset[0])[None, None, :], (slab_rows, 1, KB))
        running = absorb(
            running, block_state(query_heads, key_blocks, value_blocks, visible, score_scale)
        )
    own_index = device_rank * own_rows + jnp.arange(own_rows, dtype=jnp.int32)
    largest, weight_sum, weighted = running
    quotient = (weighted / jnp.maximum(weight_sum, 1.0)[..., None]).astype(jnp.bfloat16)
    parts_quotient = lax.all_to_all(
        quotient.reshape(1, slab_rows, head_count * DH),
        "ctx",
        split_axis=1,
        concat_axis=0,
        tiled=True,
    )
    parts_sum, parts_largest = (
        lax.all_to_all(weight_sum[None], "ctx", split_axis=1, concat_axis=0, tiled=True),
        lax.all_to_all(largest[None], "ctx", split_axis=1, concat_axis=0, tiled=True),
    )
    own_largest = jnp.max(parts_largest, axis=0)
    factors = jnp.exp(parts_largest - own_largest[None]) * parts_sum
    own_sum = jnp.sum(factors, axis=0)
    own_weighted = jnp.sum(
        factors[..., None]
        * parts_quotient.reshape(device_count, own_rows, head_count, DH).astype(jnp.float32),
        axis=0,
    )
    own_state = (own_largest, own_sum, own_weighted)
    own_queries = queries.reshape(own_rows, head_count, DH)
    keys_piece = lax.all_gather(slab_keys, "ctx", axis=0, tiled=True)
    values_piece = lax.all_gather(slab_values, "ctx", axis=0, tiled=True)
    piece_rows = keys_piece.shape[0]
    piece_blocks = piece_rows // own_rows
    key_index = jnp.arange(piece_rows, dtype=jnp.int32).reshape(piece_blocks, own_rows)
    visible = (key_index[None] <= own_index[:, None, None]) & (key_index[None] < slab_len[0])
    own_state = absorb(
        own_state,
        block_state(
            own_queries,
            keys_piece.reshape(piece_blocks, own_rows, head_count, DH),
            values_piece.reshape(piece_blocks, own_rows, head_count, DH),
            visible,
            score_scale,
        ),
    )
    final_largest, final_sum, final_weighted = own_state
    combined = (final_weighted / final_sum[..., None]).reshape(own_rows, head_count * DH)
    combined = jnp.where((own_index < slab_len[0])[:, None], combined, 0.0)
    return combined.astype(jnp.bfloat16)


def solution(mesh):
    placed = (
        P(("groups", "ctx"), None),
        P(("groups", "ctx"), None),
        P(("groups", "ctx"), None),
        P(("groups", "ctx"), None),
        P(("groups", "ctx"), None),
        P("groups"),
        P("groups"),
    )
    return jax.shard_map(
        body, mesh=mesh, in_specs=placed, out_specs=P(("groups", "ctx"), None), check_vma=False
    )
```

profile of v0, /device:TPU:0, one launch (start us, length us, event | category | flops | bytes accessed | tf_op | source)
XLA Modules:
  0.0 140.0 jit_solution(13504468689925622335)
XLA Ops:
  0.7 1.7 %fusion.59 = (bf16[256,2048]{1,0:T(8,128)(2,1)S(1)}, bf16[256,2048]{1,0:T(8,128)(2,1)S(1)}) fusion(bf16[512,2048]{1,0:T(8,128)(2,1)} %param.10), kind=kLoop, calls=%fused_computation.94 | loop fusion | bytes 4194304 | tf_op jit(solution)/shard_map/slice | solution.py:56
  2.3 0.5 copy.95
  2.9 0.2 copy-done.5
  3.1 24.6 %all_gather.9 = bf16[128,2048]{1,0:T(8,128)(2,1)S(1)} all-gather(bf16[8,2048]{1,0:T(8,128)(2,1)S(1)} %copy-done.5), channel_id=1, replica_groups=mesh['groups'=2,'ctx'=16] {'ctx'}, dimensions={0}, use_global_device_ids=true | all-gather | bytes 557056 | tf_op jit(solution)/shard_map/all_gather | solution.py:47
  27.7 0.3 copy.62
  28.0 1.3 copy.96
  29.3 0.6 fusion.3
  29.9 0.5 fusion.7
  30.5 0.6 fusion
  31.3 0.5 fusion.9
  31.9 0.5 broadcast.194
  32.3 0.7 reduce.7
  33.0 0.7 reshape.418
  33.7 3.5 %all-to-all-start = ((f32[16,1,128]{2,1,0:T(1,128)}), f32[16,1,128]{2,1,0:T(1,128)S(1)}, u32[]{:S(2)}, u32[]{:S(2)}) async-start(f32[16,1,128]{2,1,0:T(1,128)} %reshape.418), calls=%async_computation | async-start | bytes 16384 | tf_op jit(solution)/shard_map/all_to_all | solution.py:75
  37.9 23.2 %all_gather.10 = bf16[128,2048]{1,0:T(8,128)(2,1)S(1)} all-gather(bf16[8,2048]{1,0:T(8,128)(2,1)S(1)} %copy-done.4), channel_id=1, replica_groups=mesh['groups'=2,'ctx'=16] {'ctx'}, dimensions={0}, use_global_device_ids=true | all-gather | bytes 557056 | tf_op jit(solution)/shard_map/all_gather | solution.py:87
  61.2 0.9 copy.112
  62.1 3.1 %fusion.58 = (bf16[256,2048]{1,0:T(8,128)(2,1)}, bf16[256,2048]{1,0:T(8,128)(2,1)}) fusion(bf16[512,2048]{1,0:T(8,128)(2,1)} %param.11), kind=kLoop, calls=%fused_computation.93 | loop fusion | bytes 4194304 | tf_op jit(solution)/shard_map/slice | solution.py:57
  65.1 1.5 %copy.71 = bf16[256,2048]{0,1:T(8,128)(2,1)S(1)} copy(bf16[256,2048]{1,0:T(8,128)(2,1)} %get-tuple-element.16) | data formatting | bytes 2097152 | tf_op jit(solution)/shard_map/slice | solution.py:57
  66.6 3.3 %fusion.12 = f32[128,1,16,128]{0,3,2,1:T(8,128)} fusion(bf16[256,16,128]{0,2,1:T(8,128)(2,1)S(1)} %bitcast.143, f32[16,256,128]{2,1,0:T(8,128)} %copy-done, f32[128,16]{0,1:T(8,128)S(1)} %get-tuple-element.29, pred[256]{0:T(512)(128)(4,1)S(1)} %get-tuple-element.32, f32[128,16]{0,1:T(8,128)S(1)} %get-tuple-element.23), kind=kOutput, calls=%fused_computation.20 | convolution fusion | flops 136577024 | bytes 4210944 | tf_op jit(solution)/shard_map/qghk,gkhd->qghd/dot_general | solution.py:22
  69.9 3.6 %copy.73 = f32[1,128,2048]{2,0,1:T(1,128)} copy(f32[1,128,2048]{1,2,0:T(8,128)} %bitcast.144) | data formatting | bytes 2097152 | tf_op jit(solution)/shard_map/reduce_sum | solution.py:35
  73.6 1.5 %copy.75 = bf16[256,2048]{0,1:T(8,128)(2,1)S(1)} copy(bf16[256,2048]{1,0:T(8,128)(2,1)} %get-tuple-element.17) | data formatting | bytes 2097152 | tf_op jit(solution)/shard_map/slice | solution.py:57
  75.0 1.8 %fusion.13 = f32[128,1,16,128]{0,3,2,1:T(8,128)} fusion(bf16[256,16,128]{0,2,1:T(8,128)(2,1)S(1)} %bitcast.145, f32[16,256,128]{2,1,0:T(8,128)S(1)} %get-tuple-element.28, f32[128,16]{0,1:T(8,128)S(1)} %get-tuple-element.27, pred[256]{0:T(512)(128)(4,1)S(1)} %get-tuple-element.31, f32[128,16]{0,1:T(8,128)S(1)} %get-tuple-element.15), kind=kOutput, calls=%fused_computation.21 | convolution fusion | flops 136577024 | bytes 4210944 | tf_op jit(solution)/shard_map/qghk,gkhd->qghd/dot_general | solution.py:22
  76.8 2.5 %copy.77 = f32[1,128,2048]{2,0,1:T(1,128)S(1)} copy(f32[1,128,2048]{1,2,0:T(8,128)} %bitcast.146) | data formatting | bytes 2097152 | tf_op jit(solution)/shard_map/reduce_sum | solution.py:35
  79.8 0.5 select_reduce_fusion
  80.3 0.3 mul.193
  80.6 0.3 mul.197
  81.0 0.3 div.29
  81.3 0.2 copy-done.1
  81.5 3.3 %fusion.60 = bf16[128,1,2048]{2,1,0:T(2,128)(2,1)S(1)} fusion(f32[1,128,2048]{2,0,1:T(1,128)S(1)} %bitcast.152, f32[1,128,2048]{2,0,1:T(1,128)S(1)} %copy.77, f32[1,128,2048]{2,0,1:T(1,128)S(1)} %bitcast.151, f32[1,128,2048]{2,0,1:T(1,128)S(1)} %bitcast.150, f32[1,128,2048]{2,0,1:T(1,128)S(1)} %copy-done.1), kind=kLoop, calls=%fused_computation.96 | loop fusion | flops 1310720 | bytes 5767168
  84.8 0.6 fusion.28
  85.5 0.7 reduce.10
  86.2 0.7 reshape.422
  86.9 3.5 %all-to-all-start.1 = ((f32[16,1,128]{2,1,0:T(1,128)}), f32[16,1,128]{2,1,0:T(1,128)S(1)}, u32[]{:S(2)}, u32[]{:S(2)}) async-start(f32[16,1,128]{2,1,0:T(1,128)} %reshape.422), calls=%async_computation.1 | async-start | bytes 16384 | tf_op jit(solution)/shard_map/all_to_all | solution.py:74
  90.4 23.4 %all_gather.11 = bf16[128,2048]{1,0:T(8,128)(2,1)S(1)} all-gather(bf16[8,2048]{1,0:T(8,128)(2,1)S(1)} %copy-done.6), channel_id=1, replica_groups=mesh['groups'=2,'ctx'=16] {'ctx'}, dimensions={0}, use_global_device_ids=true | all-gather | bytes 557056 | tf_op jit(solution)/shard_map/all_gather | solution.py:88
  113.9 0.5 broadcast.196
  114.4 3.7 %reduce.9 = bf16[128,2048]{1,0:T(8,128)(2,1)S(1)} reduce(bf16[128,1,2048]{2,1,0:T(2,128)(2,1)S(1)} %fusion.60, bf16[]{:T(256)} %broadcast.196), dimensions={1}, to_apply=%fusion.60.reduce_sub_computation | reduce | bytes 1048578
  118.1 1.3 reshape.420
  119.4 3.6 %all-to-all-start.2 = ((bf16[16,2,8192]{2,1,0:T(2,128)(2,1)}), bf16[16,2,8192]{2,1,0:T(2,128)(2,1)S(1)}, u32[]{:S(2)}, u32[]{:S(2)}) async-start(bf16[16,2,8192]{2,1,0:T(2,128)(2,1)} %reshape.420), calls=%async_computation.2 | async-start | bytes 1048576 | tf_op jit(solution)/shard_map/all_to_all | solution.py:66
  123.0 0.6 reduce.8
  123.6 0.1 reshape.419
  123.8 0.6 reduce.11
  124.3 0.1 reshape.423
  124.8 0.6 fusion.14
  125.4 11.8 %all-to-all-done.2 = bf16[16,2,8192]{2,1,0:T(2,128)(2,1)S(1)} async-done(((bf16[16,2,8192]{2,1,0:T(2,128)(2,1)}), bf16[16,2,8192]{2,1,0:T(2,128)(2,1)S(1)}, u32[]{:S(2)}, u32[]{:S(2)}) %all-to-all-start.2) | async-done | bytes 524320 | tf_op jit(solution)/shard_map/all_to_all | solution.py:66
  137.3 0.5 reshape.421
  137.8 1.1 bitcast_convert_fusion
  138.9 0.4 multiply_reduce_fusion
  139.3 0.7 fusion.33
  (37 shorter events, 1.4 us)
Async XLA Ops:
  2.3 0.8 copy-start.5
  29.3 1.2 copy-start.2
  29.9 1.4 copy-start
  31.3 6.7 %copy-start.4 = (bf16[8,2048]{1,0:T(8,128)(2,1)S(1)}, bf16[8,2048]{1,0:T(8,128)(2,1)}, u32[]{:S(2)}) copy-start(bf16[8,2048]{1,0:T(8,128)(2,1)} %param.8) | copy-start | bytes 98308
  33.7 53.2 %all-to-all-start = ((f32[16,1,128]{2,1,0:T(1,128)}), f32[16,1,128]{2,1,0:T(1,128)S(1)}, u32[]{:S(2)}, u32[]{:S(2)}) async-start(f32[16,1,128]{2,1,0:T(1,128)} %reshape.418), calls=%async_computation | async-start | bytes 16384 | tf_op jit(solution)/shard_map/all_to_all | solution.py:75
  76.8 2.9 %copy-start.3 = (bf16[16,8,16,128]{3,2,1,0:T(8,128)(2,1)S(1)}, bf16[16,8,16,128]{3,2,1,0:T(8,128)(2,1)}, u32[]{:S(2)}) copy-start(bf16[16,8,16,128]{3,2,1,0:T(8,128)(2,1)} %copy.112) | copy-start | bytes 1572868
  80.3 1.2 copy-start.1
  84.8 5.6 %copy-start.6 = (bf16[8,2048]{1,0:T(8,128)(2,1)S(1)}, bf16[8,2048]{1,0:T(8,128)(2,1)}, u32[]{:S(2)}) copy-start(bf16[8,2048]{1,0:T(8,128)(2,1)} %param.9) | copy-start | bytes 98308
  86.9 32.5 %all-to-all-start.1 = ((f32[16,1,128]{2,1,0:T(1,128)}), f32[16,1,128]{2,1,0:T(1,128)S(1)}, u32[]{:S(2)}, u32[]{:S(2)}) async-start(f32[16,1,128]{2,1,0:T(1,128)} %reshape.422), calls=%async_computation.1 | async-start | bytes 16384 | tf_op jit(solution)/shard_map/all_to_all | solution.py:74
  119.4 17.8 %all-to-all-start.2 = ((bf16[16,2,8192]{2,1,0:T(2,128)(2,1)}), bf16[16,2,8192]{2,1,0:T(2,128)(2,1)S(1)}, u32[]{:S(2)}, u32[]{:S(2)}) async-start(bf16[16,2,8192]{2,1,0:T(2,128)(2,1)} %reshape.420), calls=%async_computation.2 | async-start | bytes 1048576 | tf_op jit(solution)/shard_map/all_to_all | solution.py:66
where the time goes:
time: 141 us; the launch traced here: 140 us
  blocking collectives  71.2 us (50%)
  local copies, waits for them, and re-layouts  23.8 us (17%)
  other arithmetic  13.6 us (10%)
  waiting for transfers between devices  11.9 us (8%)
  starting transfers between devices  10.5 us (7%)
  matrix products  7.41 us (5%)
  between operations  1.62 us (1%)
    all_gather x1, blocking collectives, body(): gathered = lax.all_gather(queries, 'ctx', axis=0, tiled=True)  24.6 us
    all_gather x1, blocking collectives, body(): values_piece = lax.all_gather(slab_values, 'ctx', axis=0, tiled=True)  23.4 us
    all_gather x1, blocking collectives, body(): keys_piece = lax.all_gather(slab_keys, 'ctx', axis=0, tiled=True)  23.2 us
    all_to_all x1, waiting for transfers between devices, body(): lax.all_to_all(quotient.reshape(1, slab_rows, head_count * DH), 'ctx', sp...  11.8 us
    unnamed x5, other arithmetic  8.48 us
    unnamed x25, local copies, waits for them, and re-layouts  7.98 us
    reduce_sum x2, local copies, waits for them, and re-layouts, absorb(): jnp.sum(factors[..., None] * products, axis=1)  6.12 us
    slice x3, local copies, waits for them, and re-layouts, body(): cache_values[block_start:block_start + KB].reshape(1, KB, head_count, DH)  6.04 us
  transfers between devices with their start and end apart: 3, of which 1 were waited for; matrix products, arithmetic and copies ran while one was open for 24% of the time, Pallas kernels for 0%

commit v1 on v0

--- a/solution.py
+++ b/solution.py
@@ -6,6 +6,27 @@
 DH = 128
 KB = 256
 very_low = -1e30
+
+
+def ring_gather(value, axis, dim):
+    peers, place, rows = (lax.axis_size(axis), lax.axis_index(axis), value.shape[dim])
+    right = [(i, (i + 1) % peers) for i in range(peers)]
+    left = [(i, (i - 1) % peers) for i in range(peers)]
+    out = jnp.zeros((*value.shape[:dim], peers * rows, *value.shape[dim + 1 :]), value.dtype)
+    out = lax.dynamic_update_slice_in_dim(out, value, place * rows, axis=dim)
+    from_left = from_right = value
+    half = peers // 2
+    for turn in range(1, half + 1):
+        from_left = lax.ppermute(from_left, axis, right)
+        out = lax.dynamic_update_slice_in_dim(
+            out, from_left, (place - turn) % peers * rows, axis=dim
+        )
+        if turn < peers - half:
+            from_right = lax.ppermute(from_right, axis, left)
+            out = lax.dynamic_update_slice_in_dim(
+                out, from_right, (place + turn) % peers * rows, axis=dim
+            )
+    return out
 
 
 def block_state(query_heads, key_blocks, value_blocks, visible, score_scale):
@@ -84,7 +105,7 @@
     )
     own_state = (own_largest, own_sum, own_weighted)
     own_queries = queries.reshape(own_rows, head_count, DH)
-    keys_piece = lax.all_gather(slab_keys, "ctx", axis=0, tiled=True)
+    keys_piece = ring_gather(slab_keys, "ctx", 0)
     values_piece = lax.all_gather(slab_values, "ctx", axis=0, tiled=True)
     piece_rows = keys_piece.shape[0]
     piece_blocks = piece_rows // own_rows

time: 141 us -> 161 us (1.14)
  starting transfers between devices: 10.5 us -> 45.1 us
  blocking collectives: 71.2 us -> 45.4 us
  waiting for transfers between devices: 11.9 us -> 22.9 us
    ppermute x0 -> x15, starting transfers between devices: none -> 32.2 us  [the longest x7 31.2 us: ring_gather(): from_right = lax.ppermute(from_right, axis, left)]
    all_gather x1 -> x0, blocking collectives: 23.2 us -> none  [body(): keys_piece = lax.all_gather(slab_keys, 'ctx', axis=0, tiled=True)]
    ppermute x0 -> x15, waiting for transfers between devices: none -> 22.9 us  [the longest x8 22.9 us: ring_gather(): from_left = lax.ppermute(from_left, axis, right)]
    all_to_all x1, waiting for transfers between devices: 11.8 us -> 0.01 us  [body(): lax.all_to_all(quotient.reshape(1, slab_rows, head_count * DH), 'ctx', sp...]
    all_gather x1, blocking collectives: 24.6 us -> 20.8 us  [body(): gathered = lax.all_gather(queries, 'ctx', axis=0, tiled=True)]
    all_to_all x1, starting transfers between devices: 3.57 us -> 5.8 us  [body(): lax.all_to_all(quotient.reshape(1, slab_rows, head_count * DH), 'ctx', sp...]
    unnamed x25 -> x29, local copies, waits for them, and re-layouts: 7.98 us -> 7.35 us
  transfers between devices with their start and end apart: 3 -> 18, of which waited for: 1 -> 7; matrix products, arithmetic and copies ran while one was open for 24% -> 26% of each run, Pallas kernels for 0% -> 0%
where the time goes in v1:
time: 161 us
  blocking collectives  45.4 us (28%)
  starting transfers between devices  45.1 us (28%)
  local copies, waits for them, and re-layouts  23.3 us (14%)
  waiting for transfers between devices  22.9 us (14%)
  other arithmetic  14.4 us (9%)
  matrix products  7.41 us (5%)
  between operations  1.98 us (1%)
    ppermute x7, starting transfers between devices, ring_gather(): from_right = lax.ppermute(from_right, axis, left)  31.2 us
    all_gather x1, blocking collectives, body(): values_piece = lax.all_gather(slab_values, 'ctx', axis=0, tiled=True)  24.6 us
    ppermute x8, waiting for transfers between devices, ring_gather(): from_left = lax.ppermute(from_left, axis, right)  22.9 us
    all_gather x1, blocking collectives, body(): gathered = lax.all_gather(queries, 'ctx', axis=0, tiled=True)  20.8 us
    unnamed x5, other arithmetic  9.17 us
    unnamed x29, local copies, waits for them, and re-layouts  7.35 us
    reduce_sum x2, local copies, waits for them, and re-layouts, absorb(): jnp.sum(factors[..., None] * products, axis=1)  6.07 us
    slice x3, local copies, waits for them, and re-layouts, body(): cache_values[block_start:block_start + KB].reshape(1, KB, head_count, DH)  6.04 us
  transfers between devices with their start and end apart: 18, of which 7 were waited for; matrix products, arithmetic and copies ran while one was open for 26% of the time, Pallas kernels for 0%

profile of v1, /device:TPU:0, one launch (start us, length us, event | category | flops | bytes accessed | tf_op | source)
XLA Modules:
  0.0 160.5 jit_solution(4372869000990651151)
XLA Ops:
  0.5 5.0 %collective-permute-start.1 = (bf16[8,2048]{1,0:T(8,128)(2,1)}, bf16[8,2048]{1,0:T(8,128)(2,1)S(1)}, u32[]{:S(2)}, u32[]{:S(2)}) collective-permute-start(bf16[8,2048]{1,0:T(8,128)(2,1)} %param.8), channel_id=1, source_target_pairs={{0,15},{1,0},{2,1},{3,2},{4,3},{5,4},{6,5},{7,6},{8,7},{9,8},{10,9... | collective-permute-start | bytes 98312 | tf_op jit(solution)/shard_map/ppermute | solution.py:25
  6.1 1.7 %fusion.59 = (bf16[256,2048]{1,0:T(8,128)(2,1)S(1)}, bf16[256,2048]{1,0:T(8,128)(2,1)S(1)}) fusion(bf16[512,2048]{1,0:T(8,128)(2,1)} %param.10), kind=kLoop, calls=%fused_computation.110 | loop fusion | bytes 4194304 | tf_op jit(solution)/shard_map/slice | solution.py:77
  7.9 0.5 copy.95
  8.6 20.8 %all_gather.6 = bf16[128,2048]{1,0:T(8,128)(2,1)S(1)} all-gather(bf16[8,2048]{1,0:T(8,128)(2,1)S(1)} %copy-done.7), channel_id=1, replica_groups=mesh['groups'=2,'ctx'=16] {'ctx'}, dimensions={0}, use_global_device_ids=true | all-gather | bytes 557056 | tf_op jit(solution)/shard_map/all_gather | solution.py:68
  29.7 1.3 copy.96
  31.0 0.6 fusion.3
  32.3 0.6 fusion
  33.6 0.5 broadcast.209
  34.1 0.8 reduce.7
  34.9 0.7 reshape.418
  35.6 3.5 %all-to-all-start = ((f32[16,1,128]{2,1,0:T(1,128)}), f32[16,1,128]{2,1,0:T(1,128)S(1)}, u32[]{:S(2)}, u32[]{:S(2)}) async-start(f32[16,1,128]{2,1,0:T(1,128)} %reshape.418), calls=%async_computation | async-start | bytes 16384 | tf_op jit(solution)/shard_map/all_to_all | solution.py:96
  39.8 3.1 %fusion.58 = (bf16[256,2048]{1,0:T(8,128)(2,1)}, bf16[256,2048]{1,0:T(8,128)(2,1)}) fusion(bf16[512,2048]{1,0:T(8,128)(2,1)} %param.11), kind=kLoop, calls=%fused_computation.109 | loop fusion | bytes 4194304 | tf_op jit(solution)/shard_map/slice | solution.py:78
  42.9 1.5 copy.71
  44.4 3.3 %fusion.12 = f32[128,1,16,128]{0,3,2,1:T(8,128)} fusion(bf16[256,16,128]{0,2,1:T(8,128)(2,1)S(1)} %bitcast.143, f32[16,256,128]{2,1,0:T(8,128)} %copy-done, f32[128,16]{0,1:T(8,128)S(1)} %get-tuple-element.29, pred[256]{0:T(512)(128)(4,1)S(1)} %get-tuple-element.32, f32[128,16]{0,1:T(8,128)S(1)} %get-tuple-element.23), kind=kOutput, calls=%fused_computation.20 | convolution fusion | flops 136577024 | bytes 4210944 | tf_op jit(solution)/shard_map/qghk,gkhd->qghd/dot_general | solution.py:43
  47.7 3.6 %copy.73 = f32[1,128,2048]{2,0,1:T(1,128)} copy(f32[1,128,2048]{1,2,0:T(8,128)} %bitcast.144) | data formatting | bytes 2097152 | tf_op jit(solution)/shard_map/reduce_sum | solution.py:56
  51.3 1.5 copy.75
  52.8 1.8 %fusion.13 = f32[128,1,16,128]{0,3,2,1:T(8,128)} fusion(bf16[256,16,128]{0,2,1:T(8,128)(2,1)S(1)} %bitcast.145, f32[16,256,128]{2,1,0:T(8,128)S(1)} %get-tuple-element.28, f32[128,16]{0,1:T(8,128)S(1)} %get-tuple-element.27, pred[256]{0:T(512)(128)(4,1)S(1)} %get-tuple-element.31, f32[128,16]{0,1:T(8,128)S(1)} %get-tuple-element.15), kind=kOutput, calls=%fused_computation.21 | convolution fusion | flops 136577024 | bytes 4210944 | tf_op jit(solution)/shard_map/qghk,gkhd->qghd/dot_general | solution.py:43
  54.6 2.5 %copy.77 = f32[1,128,2048]{2,0,1:T(1,128)S(1)} copy(f32[1,128,2048]{1,2,0:T(8,128)} %bitcast.146) | data formatting | bytes 2097152 | tf_op jit(solution)/shard_map/reduce_sum | solution.py:56
  57.3 24.6 %all_gather.7 = bf16[128,2048]{1,0:T(8,128)(2,1)} all-gather(bf16[8,2048]{1,0:T(8,128)(2,1)S(1)} %copy-done.6), channel_id=1, replica_groups=mesh['groups'=2,'ctx'=16] {'ctx'}, dimensions={0}, use_global_device_ids=true | all-gather | bytes 557056 | tf_op jit(solution)/shard_map/all_gather | solution.py:109
  83.3 3.8 %fusion.60 = bf16[128,1,2048]{2,1,0:T(2,128)(2,1)S(1)} fusion(f32[1,128,2048]{2,0,1:T(1,128)S(1)} %bitcast.152, f32[1,128,2048]{2,0,1:T(1,128)S(1)} %copy.77, f32[1,128,2048]{2,0,1:T(1,128)S(1)} %bitcast.151, f32[1,128,2048]{2,0,1:T(1,128)S(1)} %bitcast.150, f32[1,128,2048]{2,0,1:T(1,128)S(1)} %copy-done.1), kind=kLoop, calls=%fused_computation.112 | loop fusion | flops 1310720 | bytes 5767168
  87.3 0.8 reduce.10
  88.1 0.7 reshape.422
  88.8 3.7 %all-to-all-start.1 = ((f32[16,1,128]{2,1,0:T(1,128)}), f32[16,1,128]{2,1,0:T(1,128)S(1)}, u32[]{:S(2)}, u32[]{:S(2)}) async-start(f32[16,1,128]{2,1,0:T(1,128)} %reshape.422), calls=%async_computation.1 | async-start | bytes 16384 | tf_op jit(solution)/shard_map/all_to_all | solution.py:95
  92.8 0.5 broadcast.211
  93.3 3.7 %reduce.9 = bf16[128,2048]{1,0:T(8,128)(2,1)S(1)} reduce(bf16[128,1,2048]{2,1,0:T(2,128)(2,1)S(1)} %fusion.60, bf16[]{:T(256)} %broadcast.211), dimensions={1}, to_apply=%fusion.60.reduce_sub_computation | reduce | bytes 1048578
  97.0 1.3 reshape.420
  98.3 0.6 reduce.8
  99.1 5.8 %all-to-all-start.2 = ((bf16[16,2,8192]{2,1,0:T(2,128)(2,1)}), bf16[16,2,8192]{2,1,0:T(2,128)(2,1)S(1)}, u32[]{:S(2)}, u32[]{:S(2)}) async-start(bf16[16,2,8192]{2,1,0:T(2,128)(2,1)} %reshape.420), calls=%async_computation.2 | async-start | bytes 1048576 | tf_op jit(solution)/shard_map/all_to_all | solution.py:87
  104.9 0.6 reduce.11
  106.3 4.0 %collective-permute-start.3 = (bf16[8,2048]{1,0:T(8,128)(2,1)S(1)}, bf16[8,2048]{1,0:T(8,128)(2,1)S(1)}, u32[]{:S(2)}, u32[]{:S(2)}) collective-permute-start(bf16[8,2048]{1,0:T(8,128)(2,1)S(1)} %collective-permute-done.1), channel_id=1, source_target_pairs={{0,15},{1,0},{2,1},{3,2},{4,3},{5,4},{6,5},{7,6},{8,7},{9,8},{10,9... | collective-permute-start | bytes 98312 | tf_op jit(solution)/shard_map/ppermute | solution.py:25
  110.3 9.0 %collective-permute-done.2 = bf16[8,2048]{1,0:T(8,128)(2,1)S(1)} collective-permute-done((bf16[8,2048]{1,0:T(8,128)(2,1)S(1)}, bf16[8,2048]{1,0:T(8,128)(2,1)S(1)}, u32[]{:S(2)}, u32[]{:S(2)}) %collective-permute-start.2) | collective-permute-done | bytes 32800 | tf_op jit(solution)/shard_map/ppermute | solution.py:20
  119.3 4.4 %collective-permute-start.5 = (bf16[8,2048]{1,0:T(8,128)(2,1)S(1)}, bf16[8,2048]{1,0:T(8,128)(2,1)S(1)}, u32[]{:S(2)}, u32[]{:S(2)}) collective-permute-start(bf16[8,2048]{1,0:T(8,128)(2,1)S(1)} %collective-permute-done.3), channel_id=1, source_target_pairs={{0,15},{1,0},{2,1},{3,2},{4,3},{5,4},{6,5},{7,6},{8,7},{9,8},{10,9... | collective-permute-start | bytes 98312 | tf_op jit(solution)/shard_map/ppermute | solution.py:25
  123.8 1.6 collective-permute-done.4
  125.4 4.4 %collective-permute-start.7 = (bf16[8,2048]{1,0:T(8,128)(2,1)S(1)}, bf16[8,2048]{1,0:T(8,128)(2,1)S(1)}, u32[]{:S(2)}, u32[]{:S(2)}) collective-permute-start(bf16[8,2048]{1,0:T(8,128)(2,1)S(1)} %collective-permute-done.5), channel_id=1, source_target_pairs={{0,15},{1,0},{2,1},{3,2},{4,3},{5,4},{6,5},{7,6},{8,7},{9,8},{10,9... | collective-permute-start | bytes 98312 | tf_op jit(solution)/shard_map/ppermute | solution.py:25
  129.8 1.6 collective-permute-done.6
  131.4 4.4 %collective-permute-start.9 = (bf16[8,2048]{1,0:T(8,128)(2,1)S(1)}, bf16[8,2048]{1,0:T(8,128)(2,1)S(1)}, u32[]{:S(2)}, u32[]{:S(2)}) collective-permute-start(bf16[8,2048]{1,0:T(8,128)(2,1)S(1)} %collective-permute-done.7), channel_id=1, source_target_pairs={{0,15},{1,0},{2,1},{3,2},{4,3},{5,4},{6,5},{7,6},{8,7},{9,8},{10,9... | collective-permute-start | bytes 98312 | tf_op jit(solution)/shard_map/ppermute | solution.py:25
  135.9 1.6 collective-permute-done.8
  137.5 4.4 %collective-permute-start.11 = (bf16[8,2048]{1,0:T(8,128)(2,1)S(1)}, bf16[8,2048]{1,0:T(8,128)(2,1)S(1)}, u32[]{:S(2)}, u32[]{:S(2)}) collective-permute-start(bf16[8,2048]{1,0:T(8,128)(2,1)S(1)} %collective-permute-done.9), channel_id=1, source_target_pairs={{0,15},{1,0},{2,1},{3,2},{4,3},{5,4},{6,5},{7,6},{8,7},{9,8},{10,9... | collective-permute-start | bytes 98312 | tf_op jit(solution)/shard_map/ppermute | solution.py:25
  141.9 1.6 collective-permute-done.10
  143.5 4.4 %collective-permute-start.13 = (bf16[8,2048]{1,0:T(8,128)(2,1)S(1)}, bf16[8,2048]{1,0:T(8,128)(2,1)S(1)}, u32[]{:S(2)}, u32[]{:S(2)}) collective-permute-start(bf16[8,2048]{1,0:T(8,128)(2,1)S(1)} %collective-permute-done.11), channel_id=1, source_target_pairs={{0,15},{1,0},{2,1},{3,2},{4,3},{5,4},{6,5},{7,6},{8,7},{9,8},{10,9... | collective-permute-start | bytes 98312 | tf_op jit(solution)/shard_map/ppermute | solution.py:25
  148.0 1.6 collective-permute-done.12
  149.6 6.0 %collective-permute-done.14 = bf16[8,2048]{1,0:T(8,128)(2,1)S(1)} collective-permute-done((bf16[8,2048]{1,0:T(8,128)(2,1)S(1)}, bf16[8,2048]{1,0:T(8,128)(2,1)S(1)}, u32[]{:S(2)}, u32[]{:S(2)}) %collective-permute-start.14) | collective-permute-done | bytes 32800 | tf_op jit(solution)/shard_map/ppermute | solution.py:20
  155.7 0.5 select_reduce_fusion
  156.2 0.6 fusion.28
  157.2 0.6 fusion.14
  157.8 0.5 reshape.421
  158.3 1.1 bitcast_convert_fusion
  159.9 0.7 fusion.33
  (87 shorter events, 6.0 us)
Async XLA Ops:
  0.0 105.8 %collective-permute-start = (bf16[8,2048]{1,0:T(8,128)(2,1)}, bf16[8,2048]{1,0:T(8,128)(2,1)S(1)}, u32[]{:S(2)}, u32[]{:S(2)}) collective-permute-start(bf16[8,2048]{1,0:T(8,128)(2,1)} %param.8), channel_id=1, source_target_pairs={{0,1},{1,2},{2,3},{3,4},{4,5},{5,6},{6,7},{7,8},{8,9},{9,10},{10,1... | collective-permute-start | bytes 98312 | tf_op jit(solution)/shard_map/ppermute | solution.py:20
  0.5 105.8 %collective-permute-start.1 = (bf16[8,2048]{1,0:T(8,128)(2,1)}, bf16[8,2048]{1,0:T(8,128)(2,1)S(1)}, u32[]{:S(2)}, u32[]{:S(2)}) collective-permute-start(bf16[8,2048]{1,0:T(8,128)(2,1)} %param.8), channel_id=1, source_target_pairs={{0,15},{1,0},{2,1},{3,2},{4,3},{5,4},{6,5},{7,6},{8,7},{9,8},{10,9... | collective-permute-start | bytes 98312 | tf_op jit(solution)/shard_map/ppermute | solution.py:25
  7.9 0.8 copy-start.7
  31.0 1.2 copy-start.2
  31.6 1.4 copy-start
  35.6 53.2 %all-to-all-start = ((f32[16,1,128]{2,1,0:T(1,128)}), f32[16,1,128]{2,1,0:T(1,128)S(1)}, u32[]{:S(2)}, u32[]{:S(2)}) async-start(f32[16,1,128]{2,1,0:T(1,128)} %reshape.418), calls=%async_computation | async-start | bytes 16384 | tf_op jit(solution)/shard_map/all_to_all | solution.py:96
  54.6 2.8 %copy-start.6 = (bf16[8,2048]{1,0:T(8,128)(2,1)S(1)}, bf16[8,2048]{1,0:T(8,128)(2,1)}, u32[]{:S(2)}) copy-start(bf16[8,2048]{1,0:T(8,128)(2,1)} %param.9) | copy-start | bytes 98308
  54.6 27.4 %copy-start.8 = (bf16[8,2048]{1,0:T(8,128)(2,1)S(1)}, bf16[8,2048]{1,0:T(8,128)(2,1)}, u32[]{:S(2)}) copy-start(bf16[8,2048]{1,0:T(8,128)(2,1)} %param.8) | copy-start | bytes 98308
  81.9 1.4 copy-start.1
  82.0 1.0 copy-start.3
  88.8 10.3 %all-to-all-start.1 = ((f32[16,1,128]{2,1,0:T(1,128)}), f32[16,1,128]{2,1,0:T(1,128)S(1)}, u32[]{:S(2)}, u32[]{:S(2)}) async-start(f32[16,1,128]{2,1,0:T(1,128)} %reshape.422), calls=%async_computation.1 | async-start | bytes 16384 | tf_op jit(solution)/shard_map/all_to_all | solution.py:95
  92.7 17.6 %copy-start.4 = (bf16[128,2048]{1,0:T(8,128)(2,1)S(1)}, bf16[128,2048]{1,0:T(8,128)(2,1)}, u32[]{:S(2)}) copy-start(bf16[128,2048]{1,0:T(8,128)(2,1)} %copy-done.3) | copy-start | bytes 1572868
  99.1 58.6 %all-to-all-start.2 = ((bf16[16,2,8192]{2,1,0:T(2,128)(2,1)}), bf16[16,2,8192]{2,1,0:T(2,128)(2,1)S(1)}, u32[]{:S(2)}, u32[]{:S(2)}) async-start(bf16[16,2,8192]{2,1,0:T(2,128)(2,1)} %reshape.420), calls=%async_computation.2 | async-start | bytes 1048576 | tf_op jit(solution)/shard_map/all_to_all | solution.py:87
  105.8 13.5 %collective-permute-start.2 = (bf16[8,2048]{1,0:T(8,128)(2,1)S(1)}, bf16[8,2048]{1,0:T(8,128)(2,1)S(1)}, u32[]{:S(2)}, u32[]{:S(2)}) collective-permute-start(bf16[8,2048]{1,0:T(8,128)(2,1)S(1)} %collective-permute-done), channel_id=1, source_target_pairs={{0,1},{1,2},{2,3},{3,4},{4,5},{5,6},{6,7},{7,8},{8,9},{9,10},{10,1... | collective-permute-start | bytes 98312 | tf_op jit(solution)/shard_map/ppermute | solution.py:20
  106.3 13.1 %collective-permute-start.3 = (bf16[8,2048]{1,0:T(8,128)(2,1)S(1)}, bf16[8,2048]{1,0:T(8,128)(2,1)S(1)}, u32[]{:S(2)}, u32[]{:S(2)}) collective-permute-start(bf16[8,2048]{1,0:T(8,128)(2,1)S(1)} %collective-permute-done.1), channel_id=1, source_target_pairs={{0,15},{1,0},{2,1},{3,2},{4,3},{5,4},{6,5},{7,6},{8,7},{9,8},{10,9... | collective-permute-start | bytes 98312 | tf_op jit(solution)/shard_map/ppermute | solution.py:25
  119.3 6.0 %collective-permute-start.4 = (bf16[8,2048]{1,0:T(8,128)(2,1)S(1)}, bf16[8,2048]{1,0:T(8,128)(2,1)S(1)}, u32[]{:S(2)}, u32[]{:S(2)}) collective-permute-start(bf16[8,2048]{1,0:T(8,128)(2,1)S(1)} %collective-permute-done.2), channel_id=1, source_target_pairs={{0,1},{1,2},{2,3},{3,4},{4,5},{5,6},{6,7},{7,8},{8,9},{9,10},{10,1... | collective-permute-start | bytes 98312 | tf_op jit(solution)/shard_map/ppermute | solution.py:20
  119.3 6.0 %collective-permute-start.5 = (bf16[8,2048]{1,0:T(8,128)(2,1)S(1)}, bf16[8,2048]{1,0:T(8,128)(2,1)S(1)}, u32[]{:S(2)}, u32[]{:S(2)}) collective-permute-start(bf16[8,2048]{1,0:T(8,128)(2,1)S(1)} %collective-permute-done.3), channel_id=1, source_target_pairs={{0,15},{1,0},{2,1},{3,2},{4,3},{5,4},{6,5},{7,6},{8,7},{9,8},{10,9... | collective-permute-start | bytes 98312 | tf_op jit(solution)/shard_map/ppermute | solution.py:25
  125.4 6.0 %collective-permute-start.6 = (bf16[8,2048]{1,0:T(8,128)(2,1)S(1)}, bf16[8,2048]{1,0:T(8,128)(2,1)S(1)}, u32[]{:S(2)}, u32[]{:S(2)}) collective-permute-start(bf16[8,2048]{1,0:T(8,128)(2,1)S(1)} %collective-permute-done.4), channel_id=1, source_target_pairs={{0,1},{1,2},{2,3},{3,4},{4,5},{5,6},{6,7},{7,8},{8,9},{9,10},{10,1... | collective-permute-start | bytes 98312 | tf_op jit(solution)/shard_map/ppermute | solution.py:20
  125.4 6.0 %collective-permute-start.7 = (bf16[8,2048]{1,0:T(8,128)(2,1)S(1)}, bf16[8,2048]{1,0:T(8,128)(2,1)S(1)}, u32[]{:S(2)}, u32[]{:S(2)}) collective-permute-start(bf16[8,2048]{1,0:T(8,128)(2,1)S(1)} %collective-permute-done.5), channel_id=1, source_target_pairs={{0,15},{1,0},{2,1},{3,2},{4,3},{5,4},{6,5},{7,6},{8,7},{9,8},{10,9... | collective-permute-start | bytes 98312 | tf_op jit(solution)/shard_map/ppermute | solution.py:25
  131.4 6.0 %collective-permute-start.8 = (bf16[8,2048]{1,0:T(8,128)(2,1)S(1)}, bf16[8,2048]{1,0:T(8,128)(2,1)S(1)}, u32[]{:S(2)}, u32[]{:S(2)}) collective-permute-start(bf16[8,2048]{1,0:T(8,128)(2,1)S(1)} %collective-permute-done.6), channel_id=1, source_target_pairs={{0,1},{1,2},{2,3},{3,4},{4,5},{5,6},{6,7},{7,8},{8,9},{9,10},{10,1... | collective-permute-start | bytes 98312 | tf_op jit(solution)/shard_map/ppermute | solution.py:20
  131.4 6.0 %collective-permute-start.9 = (bf16[8,2048]{1,0:T(8,128)(2,1)S(1)}, bf16[8,2048]{1,0:T(8,128)(2,1)S(1)}, u32[]{:S(2)}, u32[]{:S(2)}) collective-permute-start(bf16[8,2048]{1,0:T(8,128)(2,1)S(1)} %collective-permute-done.7), channel_id=1, source_target_pairs={{0,15},{1,0},{2,1},{3,2},{4,3},{5,4},{6,5},{7,6},{8,7},{9,8},{10,9... | collective-permute-start | bytes 98312 | tf_op jit(solution)/shard_map/ppermute | solution.py:25
  137.5 6.0 %collective-permute-start.10 = (bf16[8,2048]{1,0:T(8,128)(2,1)S(1)}, bf16[8,2048]{1,0:T(8,128)(2,1)S(1)}, u32[]{:S(2)}, u32[]{:S(2)}) collective-permute-start(bf16[8,2048]{1,0:T(8,128)(2,1)S(1)} %collective-permute-done.8), channel_id=1, source_target_pairs={{0,1},{1,2},{2,3},{3,4},{4,5},{5,6},{6,7},{7,8},{8,9},{9,10},{10,1... | collective-permute-start | bytes 98312 | tf_op jit(solution)/shard_map/ppermute | solution.py:20
  137.5 6.0 %collective-permute-start.11 = (bf16[8,2048]{1,0:T(8,128)(2,1)S(1)}, bf16[8,2048]{1,0:T(8,128)(2,1)S(1)}, u32[]{:S(2)}, u32[]{:S(2)}) collective-permute-start(bf16[8,2048]{1,0:T(8,128)(2,1)S(1)} %collective-permute-done.9), channel_id=1, source_target_pairs={{0,15},{1,0},{2,1},{3,2},{4,3},{5,4},{6,5},{7,6},{8,7},{9,8},{10,9... | collective-permute-start | bytes 98312 | tf_op jit(solution)/shard_map/ppermute | solution.py:25
  143.5 6.0 %collective-permute-start.12 = (bf16[8,2048]{1,0:T(8,128)(2,1)S(1)}, bf16[8,2048]{1,0:T(8,128)(2,1)S(1)}, u32[]{:S(2)}, u32[]{:S(2)}) collective-permute-start(bf16[8,2048]{1,0:T(8,128)(2,1)S(1)} %collective-permute-done.10), channel_id=1, source_target_pairs={{0,1},{1,2},{2,3},{3,4},{4,5},{5,6},{6,7},{7,8},{8,9},{9,10},{10,1... | collective-permute-start | bytes 98312 | tf_op jit(solution)/shard_map/ppermute | solution.py:20
  143.5 6.0 %collective-permute-start.13 = (bf16[8,2048]{1,0:T(8,128)(2,1)S(1)}, bf16[8,2048]{1,0:T(8,128)(2,1)S(1)}, u32[]{:S(2)}, u32[]{:S(2)}) collective-permute-start(bf16[8,2048]{1,0:T(8,128)(2,1)S(1)} %collective-permute-done.11), channel_id=1, source_target_pairs={{0,15},{1,0},{2,1},{3,2},{4,3},{5,4},{6,5},{7,6},{8,7},{9,8},{10,9... | collective-permute-start | bytes 98312 | tf_op jit(solution)/shard_map/ppermute | solution.py:25
  149.5 6.0 %collective-permute-start.14 = (bf16[8,2048]{1,0:T(8,128)(2,1)S(1)}, bf16[8,2048]{1,0:T(8,128)(2,1)S(1)}, u32[]{:S(2)}, u32[]{:S(2)}) collective-permute-start(bf16[8,2048]{1,0:T(8,128)(2,1)S(1)} %collective-permute-done.12), channel_id=1, source_target_pairs={{0,1},{1,2},{2,3},{3,4},{4,5},{5,6},{6,7},{7,8},{8,9},{9,10},{10,1... | collective-permute-start | bytes 98312 | tf_op jit(solution)/shard_map/ppermute | solution.py:20
  155.7 1.5 copy-start.5
